TPU v7x, 32 devices: a whole 2x2x4 slice. The times are simulated.
32 devices in a mesh: unit: 2 (over core), zero: 4 (over z), model: 4 (over y, x).
Axes of the slice: x: 2, y: 2, z: 4, core: 2. Of those that a mesh axis runs over, the one named last changes fastest.
Arguments:
- first_query: float32 [16384, 8192], P(('unit', 'zero'), 'model'), parts along dimension 0, may hold values from -0.09375 to 0.09375
- second_query: float32 [16384, 8192], P(('unit', 'zero'), 'model'), parts along dimension 0, may hold values from -0.0625 to 0.0625
- first_key: float32 [16384, 1024], P(('unit', 'zero'), 'model'), parts along dimension 0, may hold values from -0.09375 to 0.09375
- second_key: float32 [16384, 1024], P(('unit', 'zero'), 'model'), parts along dimension 0, may hold values from -0.0625 to 0.0625
- first_value: float32 [16384, 1024], P(('unit', 'zero'), 'model'), parts along dimension 0, may hold values from -0.09375 to 0.09375
- second_value: float32 [16384, 1024], P(('unit', 'zero'), 'model'), parts along dimension 0, may hold values from -0.0625 to 0.0625
- mix_share: float32 [16384], P(('unit', 'zero')), parts along dimension 0, may hold values from 0.2 to 0.8
- norm_train: float32 [16384], P(('unit', 'zero', 'model')), parts along dimension 0, may hold values from 0.25 to 1.75
- norm_step: float32 [16384], P(('unit', 'zero', 'model')), parts along dimension 0, may hold values from -0.3 to 0.3
Outputs:
- serve_query: bfloat16 [16384, 8192], P('unit', 'model'), parts along dimension 0
- serve_key: bfloat16 [16384, 1024], P('unit', 'model'), parts along dimension 0
- serve_value: bfloat16 [16384, 1024], P('unit', 'model'), parts along dimension 0
- factor_query: float32 [16384], P(('unit', 'model')), parts along dimension 0
- factor_key: float32 [2048], P(('unit', 'model')), parts along dimension 0
- factor_value: float32 [2048], P(('unit', 'model')), parts along dimension 0
- serve_norm: bfloat16 [16384], P('unit'), parts along dimension 0
There are 2 independent parts, one for each index of `unit`. A program takes and returns all parts, laid end to end along the dimension named above; each array names one. Nothing has to cross between parts.
All inputs are finite; a program needn't handle non-finite values.
Results may differ from a plain program's by a relative error of at most 0.0004.
Values may be sent and summed in bfloat16 or wider, within the bound.
A program may use at most 192 MiB of HBM per device.

v0:
```python
import functools

import jax
import jax.numpy as jnp
from jax import lax
from jax.experimental import pallas as pl
from jax.experimental.pallas import tpu as pltpu
from jax.sharding import PartitionSpec as P


MESH = pl.DeviceIdType.MESH
LANES = 128
READS = 4
SHARES = (4, 4, 4, 3, 1)


def total_of(held, n_zero):
    total = held[0]
    for k in range(1, n_zero):
        total = total + held[k]
    return total


def lead_kernel(
    n_zero,
    first_key,
    second_key,
    first_value,
    second_value,
    share_ref,
    train_ref,
    step_ref,
    block_ref,
    key_total,
    value_total,
    gain_ref,
    key_a,
    key_b,
    value_a,
    value_b,
    wide,
    narrow,
    norm,
    key_held,
    value_held,
    key_part,
    value_part,
    read_sem,
    write_sem,
    sent,
    got,
    own,
):
    z = lax.axis_index("zero")
    rows, width = key_a.shape
    step = rows // READS
    barrier = pltpu.get_barrier_semaphore()
    peers = [lax.rem(z + k, n_zero) for k in range(1, n_zero)]
    for peer in peers:
        pl.semaphore_signal(barrier, inc=1, device_id={"zero": peer}, device_id_type=MESH)

    reads = []
    for which, (source, target) in enumerate(
        ((first_key, key_a), (second_key, key_b), (first_value, value_a), (second_value, value_b))
    ):
        reads.append([])
        for k in range(READS):
            part = pl.ds(k * step, step)
            reads[-1].append(pltpu.make_async_copy(source.at[part], target.at[part], read_sem.at[which, k]))
    for pair in (reads[:2], reads[2:]):
        for k in range(READS):
            for group in pair:
                group[k].start()

    norm[...] = (train_ref[...] + step_ref[...]).astype(norm.dtype)
    lanes = min(LANES, width)
    for k in range(rows // LANES):
        line = jnp.broadcast_to(share_ref[k : k + 1, :], (LANES, LANES))
        wide[k * LANES : (k + 1) * LANES, :] = jnp.transpose(line)

    def sums(first, second, groups, target):
        size = min(LANES, step)
        sums_of = [jnp.zeros((8, min(lanes, width - low)), jnp.float32) for low in range(0, width, lanes)]
        for k in range(READS):
            for group in groups:
                group[k].wait()
            for low in range(k * step, (k + 1) * step, size):
                for c in range(len(sums_of)):
                    columns = pl.ds(c * lanes, sums_of[c].shape[1])
                    here = pl.ds(low, size)
                    share = wide[here, : sums_of[c].shape[1]]
                    fresh = share * first[here, columns] + (1.0 - share) * second[here, columns]
                    first[here, columns] = fresh
                    square = fresh * fresh
                    sums_of[c] = sums_of[c] + jnp.sum(square.reshape(size // 8, 8, square.shape[1]), axis=0)
        for c, value in enumerate(sums_of):
            target[:, c * lanes : c * lanes + value.shape[1]] = jnp.sum(value, axis=0, keepdims=True)

    def exchange(index, source, target):
        copies = []
        for k, peer in enumerate(peers, 1):
            copies.append(
                pltpu.make_async_remote_copy(
                    src_ref=source,
                    dst_ref=target.at[z],
                    send_sem=sent.at[index, k],
                    recv_sem=got.at[index, k],
                    device_id={"zero": peer},
                    device_id_type=MESH,
                )
            )
        for copy in copies:
            copy.start()
        return copies

    sums(key_a, key_b, reads[:2], key_part)
    pl.semaphore_wait(barrier, n_zero - 1)
    key_copies = exchange(0, key_part, key_held)
    key_held[z] = key_part[...]
    sums(value_a, value_b, reads[2:], value_part)
    value_held[z] = value_part[...]
    mine = pltpu.make_async_copy(norm, gain_ref.at[z], own)
    mine.start()
    value_copies = exchange(1, value_part, value_held)
    norm_copies = exchange(2, norm, gain_ref)

    for copy in key_copies:
        copy.wait()
    total = total_of(key_held, n_zero)
    key_total[...] = total
    scale = 1.0 / jnp.sqrt(total)
    writes = []
    for k in range(READS):
        part = pl.ds(k * step, step)
        narrow[part, :] = (key_a[part, :] * scale).astype(narrow.dtype)
        writes.append(pltpu.make_async_copy(narrow.at[part], block_ref.at[part], write_sem.at[k]))
        writes[-1].start()
    for copy in value_copies:
        copy.wait()
    value_total[...] = total_of(value_held, n_zero)
    for copy in norm_copies + writes + [mine]:
        copy.wait()


def lead(n_zero, first_key, second_key, first_value, second_value, share, train, step):
    vmem = pl.BlockSpec(memory_space=pltpu.VMEM)
    hbm = pl.BlockSpec(memory_space=pl.ANY)
    shape = first_key.shape
    rows, width = shape
    part = (1, width)
    return pl.pallas_call(
        functools.partial(lead_kernel, n_zero),
        out_shape=(
            jax.ShapeDtypeStruct(shape, jnp.bfloat16),
            jax.ShapeDtypeStruct(part, jnp.float32),
            jax.ShapeDtypeStruct(part, jnp.float32),
            jax.ShapeDtypeStruct((n_zero,) + train.shape, jnp.bfloat16),
        ),
        in_specs=[hbm] * 4 + [vmem] * 3,
        out_specs=(hbm, vmem, vmem, vmem),
        scratch_shapes=[pltpu.VMEM(shape, jnp.float32)] * 4
        + [
            pltpu.VMEM((rows, LANES), jnp.float32),
            pltpu.VMEM(shape, jnp.bfloat16),
            pltpu.VMEM(train.shape, jnp.bfloat16),
            pltpu.VMEM((n_zero,) + part, jnp.float32),
            pltpu.VMEM((n_zero,) + part, jnp.float32),
            pltpu.VMEM(part, jnp.float32),
            pltpu.VMEM(part, jnp.float32),
            pltpu.SemaphoreType.DMA((4, READS)),
            pltpu.SemaphoreType.DMA((READS,)),
            pltpu.SemaphoreType.DMA((3, n_zero)),
            pltpu.SemaphoreType.DMA((3, n_zero)),
            pltpu.SemaphoreType.DMA,
        ],
        compiler_params=pltpu.CompilerParams(collective_id=0, has_side_effects=True),
        name="lead",
    )(first_key, second_key, first_value, second_value, share, train, step)


def spread_kernel(n_model, part_ref, all_ref, sent, got, own):
    m = lax.axis_index("model")
    barrier = pltpu.get_barrier_semaphore()
    peers = [lax.rem(m + k, n_model) for k in range(1, n_model)]
    for peer in peers:
        pl.semaphore_signal(barrier, inc=1, device_id={"model": peer}, device_id_type=MESH)
    mine = pltpu.make_async_copy(part_ref, all_ref.at[m], own)
    mine.start()
    pl.semaphore_wait(barrier, n_model - 1)
    copies = []
    for k, peer in enumerate(peers, 1):
        copies.append(
            pltpu.make_async_remote_copy(
                src_ref=part_ref,
                dst_ref=all_ref.at[m],
                send_sem=sent.at[k],
                recv_sem=got.at[k],
                device_id={"model": peer},
                device_id_type=MESH,
            )
        )
    for copy in copies:
        copy.start()
    for copy in copies + [mine]:
        copy.wait()


def spread(n_model, part):
    vmem = pl.BlockSpec(memory_space=pltpu.VMEM)
    return pl.pallas_call(
        functools.partial(spread_kernel, n_model),
        out_shape=jax.ShapeDtypeStruct((n_model,) + part.shape, part.dtype),
        in_specs=[vmem],
        out_specs=vmem,
        scratch_shapes=[
            pltpu.SemaphoreType.DMA((n_model,)),
            pltpu.SemaphoreType.DMA((n_model,)),
            pltpu.SemaphoreType.DMA,
        ],
        compiler_params=pltpu.CompilerParams(collective_id=1, has_side_effects=True),
        name="spread",
    )(part)


def piece_bounds(rows):
    bounds, low = [], 0
    for share in SHARES:
        high = low + rows * share // sum(SHARES)
        bounds.append((low, high))
        low = high
    return bounds


def merge(
    n_zero,
    n_model,
    first_query,
    second_query,
    first_key,
    second_key,
    first_value,
    second_value,
    mix_share,
    norm_train,
    norm_step,
):
    rows = mix_share.shape[0]
    z = lax.axis_index("zero")
    up = [[(k, k + 1) for k in range(hop, n_zero - 1)] for hop in range(n_zero - 1)]
    down = [[(k, k - 1) for k in range(1, n_zero - hop)] for hop in range(n_zero - 1)]
    ring = [[(k, (k + shift) % n_zero) for k in range(n_zero)] for shift in range(n_zero)]

    key_block, key_total, value_total, gain = lead(
        n_zero,
        first_key,
        second_key,
        first_value,
        second_value,
        mix_share.reshape(-1, LANES),
        norm_train[None, :],
        norm_step[None, :],
    )
    factors = [None, jnp.sqrt(key_total[0]), jnp.sqrt(value_total[0])]

    def send(block, hop):
        above = lax.ppermute(block[0], "zero", up[hop])
        below = lax.ppermute(block[1], "zero", down[hop])
        return above, below

    key_moved = send((key_block, key_block), 0)
    first_query, second_query, first_value, second_value, share, _ = lax.optimization_barrier(
        (first_query, second_query, first_value, second_value, mix_share, key_block)
    )
    share = share[:, None]
    pairs = ((first_query, second_query), None, (first_value, second_value))

    def fresh_of(which, low, high):
        first, second = pairs[which][0][low:high], pairs[which][1][low:high]
        return share[low:high] * first + (1.0 - share[low:high]) * second

    def narrow(which, low, high, after=None):
        scale = factors[which]
        if after is not None:
            scale, _ = lax.optimization_barrier((scale, after))
        block = (fresh_of(which, low, high) / scale).astype(jnp.bfloat16)
        return lax.optimization_barrier(block)

    value_block = narrow(2, 0, rows)
    fresh = fresh_of(0, 0, rows)
    part = jnp.sum(fresh * fresh, axis=0)
    part, value_block = lax.optimization_barrier((part, value_block))
    parts = [part]
    for shift in range(1, n_zero):
        parts.append(lax.ppermute(part, "zero", ring[shift]))
    stack = jnp.stack(parts)
    total = sum(
        lax.dynamic_index_in_dim(stack, lax.rem(z + n_zero - k, n_zero), 0, keepdims=False)
        for k in range(n_zero)
    )
    factors[0] = jnp.sqrt(total)

    pieces = [(1, 0, rows), (2, 0, rows)]
    pieces += [(0, low, high) for low, high in piece_bounds(rows)]
    blocks = [key_block, value_block]
    for k, piece in enumerate(pieces[2:], 2):
        blocks.append(narrow(*piece, after=blocks[-1]))
    gain, factors[1], _ = lax.optimization_barrier((gain, factors[1], blocks[-1]))
    gain = spread(n_model, gain)

    widths = [first_query.shape[1], first_key.shape[1], first_value.shape[1]]
    serve = [jnp.zeros((n_zero * rows, width), jnp.bfloat16) for width in widths]

    def place(piece, block, owner):
        which, low, _ = piece
        serve[which] = lax.dynamic_update_slice(serve[which], block, (owner * rows + low, jnp.zeros_like(owner)))

    for piece, block in zip(pieces, blocks):
        place(piece, block, z)
    above, below = {}, {}
    flying = [(block, block) for block in blocks]
    for hop in range(n_zero - 1):
        for k, piece in enumerate(pieces):
            flying[k] = key_moved if (hop, k) == (0, 0) else send(flying[k], hop)
            above[hop + 1, k], below[hop + 1, k] = flying[k]
        for k, piece in enumerate(pieces):
            for away in range(1, n_zero):
                if max(away, n_zero - away) == hop + 1:
                    block = jnp.where(z + away < n_zero, below[away, k], above[n_zero - away, k])
                    place(piece, block, lax.rem(z + away, n_zero))
    gain = gain.reshape(n_model, n_zero, -1).transpose(1, 0, 2)
    return (*serve, *factors, gain.reshape(-1))


def solution(mesh):
    in_specs = (
        P(("unit", "zero"), "model"),
        P(("unit", "zero"), "model"),
        P(("unit", "zero"), "model"),
        P(("unit", "zero"), "model"),
        P(("unit", "zero"), "model"),
        P(("unit", "zero"), "model"),
        P(("unit", "zero")),
        P(("unit", "zero", "model")),
        P(("unit", "zero", "model")),
    )
    out_specs = (
        P("unit", "model"),
        P("unit", "model"),
        P("unit", "model"),
        P(("unit", "model")),
        P(("unit", "model")),
        P(("unit", "model")),
        P("unit"),
    )
    return jax.shard_map(
        functools.partial(merge, mesh.shape["zero"], mesh.shape["model"]),
        mesh=mesh,
        in_specs=in_specs,
        out_specs=out_specs,
        check_vma=False,
    )
```

profile of v0, /device:TPU:0, one launch (start us, length us, event | category | flops | bytes accessed | tf_op | source)
XLA Modules:
  0.0 741.6 jit_solution(9754829612738793523)
XLA Ops:
  0.7 12.2 %lead.1 = (bf16[2048,256]{1,0:T(8,128)(2,1)}, f32[1,256]{1,0:T(1,128)}, f32[1,256]{1,0:T(1,128)}, bf16[4,1,512]{2,1,0:T(2,128)(2,1)}) custom-call(f32[2048,256]{1,0:T(8,128)} %first_key.1, f32[2048,256]{1,0:T(8,128)} %second_key.1, f32[2048,256]{1,0:T(8,128)} %first_value.1, f32[2048,256]{1,0:T(8,128)} %second_value.1, f32[16,128]{1,0:T(8,128)} %bitcast.24, ...), custom_call_target="tpu_custom_call" | custom-call | tf_op jit(solution)/shard_map/lead/pallas_call | solution.py:151
  15.5 11.6 %multiply_reduce_fusion = f32[2048]{0:T(1024)S(1)} fusion(f32[2048,2048]{1,0:T(8,128)} %param.10, f32[2048,2048]{1,0:T(8,128)} %param.9, f32[2048]{0:T(1024)S(1)} %broadcast_subtract_fusion, f32[2048]{0:T(1024)S(1)} %copy-done.25), kind=kLoop, calls=%fused_computation | loop fusion | flops 20969472 | bytes 33579008 | tf_op jit(solution)/shard_map/reduce_sum | solution.py:290
  29.0 2.1 collective-permute-start.2
  33.3 4.9 divide_convert_fusion.2
  38.3 4.8 divide_convert_fusion.1
  43.1 3.9 divide_convert_fusion
  47.0 3.5 divide_convert_fusion.3
  50.5 2.3 divide_convert_fusion.5
  54.2 5.5 collective-permute-start.21
  60.9 4.6 collective-permute-start.17
  65.6 4.2 collective-permute-done.19
  69.8 4.0 collective-permute-start.41
  75.1 5.6 collective-permute-start.35
  80.6 46.7 %collective-permute-done.41 = bf16[2048,256]{1,0:T(8,128)(2,1)S(1)} collective-permute-done((bf16[2048,256]{1,0:T(8,128)(2,1)S(1)}, bf16[2048,256]{1,0:T(8,128)(2,1)S(1)}, u32[]{:S(2)}, u32[]{:S(2)}) %collective-permute-start.41) | collective-permute-done | bytes 1048608 | tf_op jit(solution)/shard_map/ppermute | solution.py:266
  129.9 16.8 %collective-permute-done.35 = bf16[2048,256]{1,0:T(8,128)(2,1)} collective-permute-done((bf16[2048,256]{1,0:T(8,128)(2,1)S(1)}, bf16[2048,256]{1,0:T(8,128)(2,1)}, u32[]{:S(2)}, u32[]{:S(2)}) %collective-permute-start.35) | collective-permute-done | bytes 1048608 | tf_op jit(solution)/shard_map/ppermute | solution.py:266
  150.4 50.4 %collective-permute-done.40 = bf16[2048,256]{1,0:T(8,128)(2,1)S(1)} collective-permute-done((bf16[2048,256]{1,0:T(8,128)(2,1)}, bf16[2048,256]{1,0:T(8,128)(2,1)S(1)}, u32[]{:S(2)}, u32[]{:S(2)}) %collective-permute-start.40) | collective-permute-done | bytes 1048608 | tf_op jit(solution)/shard_map/ppermute | solution.py:267
  200.8 5.3 collective-permute-start.5
  206.2 2.6 collective-permute-start.9
  208.8 8.8 %collective-permute-done.34 = bf16[2048,256]{1,0:T(8,128)(2,1)S(1)} collective-permute-done((bf16[2048,256]{1,0:T(8,128)(2,1)S(1)}, bf16[2048,256]{1,0:T(8,128)(2,1)S(1)}, u32[]{:S(2)}, u32[]{:S(2)}) %collective-permute-start.34) | collective-permute-done | bytes 1048608 | tf_op jit(solution)/shard_map/ppermute | solution.py:267
  220.8 2.0 copy-done.3
  224.1 2.3 broadcast.41.clone
  227.5 6.1 spread.1
  235.0 11.2 %broadcast_in_dim.6 = bf16[8192,2048]{1,0:T(8,128)(2,1)} broadcast(bf16[]{:T(256)} %constant.67.clone.1), dimensions={} | broadcast | bytes 33554432 | tf_op jit(solution)/shard_map/broadcast_in_dim | solution.py:311
  246.1 3.2 constant_dynamic-update-slice_fusion.6
  249.3 5.4 collective-permute-start.13
  254.7 3.2 constant_dynamic-update-slice_fusion.5
  262.3 33.7 %collective-permute-done.9 = bf16[512,2048]{1,0:T(8,128)(2,1)} collective-permute-done((bf16[512,2048]{1,0:T(8,128)(2,1)}, bf16[512,2048]{1,0:T(8,128)(2,1)}, u32[]{:S(2)}, u32[]{:S(2)}) %collective-permute-start.9) | collective-permute-done | bytes 2097184 | tf_op jit(solution)/shard_map/ppermute | solution.py:266
  299.0 15.2 %collective-permute-done.11 = bf16[512,2048]{1,0:T(8,128)(2,1)} collective-permute-done((bf16[512,2048]{1,0:T(8,128)(2,1)S(1)}, bf16[512,2048]{1,0:T(8,128)(2,1)}, u32[]{:S(2)}, u32[]{:S(2)}) %collective-permute-start.11) | collective-permute-done | bytes 2097184 | tf_op jit(solution)/shard_map/ppermute | solution.py:267
  316.1 9.8 %collective-permute-done.13 = bf16[512,2048]{1,0:T(8,128)(2,1)S(1)} collective-permute-done((bf16[512,2048]{1,0:T(8,128)(2,1)S(1)}, bf16[512,2048]{1,0:T(8,128)(2,1)S(1)}, u32[]{:S(2)}, u32[]{:S(2)}) %collective-permute-start.13) | collective-permute-done | bytes 2097184 | tf_op jit(solution)/shard_map/ppermute | solution.py:266
  328.0 8.6 %collective-permute-done.44 = bf16[2048,256]{1,0:T(8,128)(2,1)S(1)} collective-permute-done((bf16[2048,256]{1,0:T(8,128)(2,1)S(1)}, bf16[2048,256]{1,0:T(8,128)(2,1)S(1)}, u32[]{:S(2)}, u32[]{:S(2)}) %collective-permute-start.44) | collective-permute-done | bytes 1048608 | tf_op jit(solution)/shard_map/ppermute | solution.py:267
  341.8 62.1 %collective-permute-done.38 = bf16[2048,256]{1,0:T(8,128)(2,1)S(1)} collective-permute-done((bf16[2048,256]{1,0:T(8,128)(2,1)S(1)}, bf16[2048,256]{1,0:T(8,128)(2,1)S(1)}, u32[]{:S(2)}, u32[]{:S(2)}) %collective-permute-start.38) | collective-permute-done | bytes 1048608 | tf_op jit(solution)/shard_map/ppermute | solution.py:267
  409.8 2.1 select_dynamic-update-slice_fusion.8
  411.9 36.9 %collective-permute-done.8 = bf16[512,2048]{1,0:T(8,128)(2,1)S(1)} collective-permute-done((bf16[512,2048]{1,0:T(8,128)(2,1)}, bf16[512,2048]{1,0:T(8,128)(2,1)S(1)}, u32[]{:S(2)}, u32[]{:S(2)}) %collective-permute-start.8) | collective-permute-done | bytes 2097184 | tf_op jit(solution)/shard_map/ppermute | solution.py:267
  449.7 2.1 select_dynamic-update-slice_fusion.7
  451.8 42.0 %collective-permute-done.12 = bf16[512,2048]{1,0:T(8,128)(2,1)S(1)} collective-permute-done((bf16[512,2048]{1,0:T(8,128)(2,1)}, bf16[512,2048]{1,0:T(8,128)(2,1)S(1)}, u32[]{:S(2)}, u32[]{:S(2)}) %collective-permute-start.12) | collective-permute-done | bytes 2097184 | tf_op jit(solution)/shard_map/ppermute | solution.py:267
  495.8 2.1 select_dynamic-update-slice_fusion.6
  499.2 28.3 %collective-permute-done.16 = bf16[384,2048]{1,0:T(8,128)(2,1)S(1)} collective-permute-done((bf16[384,2048]{1,0:T(8,128)(2,1)S(1)}, bf16[384,2048]{1,0:T(8,128)(2,1)S(1)}, u32[]{:S(2)}, u32[]{:S(2)}) %collective-permute-start.16) | collective-permute-done | bytes 1572896 | tf_op jit(solution)/shard_map/ppermute | solution.py:267
  530.8 45.3 %collective-permute-done.20 = bf16[128,2048]{1,0:T(8,128)(2,1)S(1)} collective-permute-done((bf16[128,2048]{1,0:T(8,128)(2,1)}, bf16[128,2048]{1,0:T(8,128)(2,1)S(1)}, u32[]{:S(2)}, u32[]{:S(2)}) %collective-permute-start.20) | collective-permute-done | bytes 524320 | tf_op jit(solution)/shard_map/ppermute | solution.py:267
  579.1 3.7 select_dynamic-update-slice_fusion.5
  584.1 2.1 select_dynamic-update-slice_fusion.4
  587.5 3.7 select_dynamic-update-slice_fusion.3
  591.2 70.2 %collective-permute-done.26 = bf16[512,2048]{1,0:T(8,128)(2,1)S(1)} collective-permute-done((bf16[512,2048]{1,0:T(8,128)(2,1)S(1)}, bf16[512,2048]{1,0:T(8,128)(2,1)S(1)}, u32[]{:S(2)}, u32[]{:S(2)}) %collective-permute-start.26) | collective-permute-done | bytes 2097184 | tf_op jit(solution)/shard_map/ppermute | solution.py:267
  662.1 2.1 select_dynamic-update-slice_fusion.2
  665.7 3.7 select_dynamic-update-slice_fusion.1
  669.4 36.9 %collective-permute-done.28 = bf16[512,2048]{1,0:T(8,128)(2,1)S(1)} collective-permute-done((bf16[512,2048]{1,0:T(8,128)(2,1)S(1)}, bf16[512,2048]{1,0:T(8,128)(2,1)S(1)}, u32[]{:S(2)}, u32[]{:S(2)}) %collective-permute-start.28) | collective-permute-done | bytes 2097184 | tf_op jit(solution)/shard_map/ppermute | solution.py:267
  706.3 2.1 select_dynamic-update-slice_fusion
  710.2 26.8 %collective-permute-done.30 = bf16[384,2048]{1,0:T(8,128)(2,1)S(1)} collective-permute-done((bf16[384,2048]{1,0:T(8,128)(2,1)S(1)}, bf16[384,2048]{1,0:T(8,128)(2,1)S(1)}, u32[]{:S(2)}, u32[]{:S(2)}) %collective-permute-start.30) | collective-permute-done | bytes 1572896 | tf_op jit(solution)/shard_map/ppermute | solution.py:267
  738.8 2.0 select_dynamic-update-slice_fusion.19
  (148 shorter events, 65.6 us)
Async XLA Ops:
  27.2 5.5 collective-permute-start
  27.8 4.9 collective-permute-start.1
  29.0 4.3 collective-permute-start.2
  31.0 44.0 %collective-permute-start.39 = (bf16[2048,256]{1,0:T(8,128)(2,1)S(1)}, bf16[2048,256]{1,0:T(8,128)(2,1)}, u32[]{:S(2)}, u32[]{:S(2)}) collective-permute-start(bf16[2048,256]{1,0:T(8,128)(2,1)S(1)} %divide_convert_fusion.4), channel_id=1, source_target_pairs={{4,0},{8,4},{12,8},{5,1},{9,5},{13,9},{6,2},{10,6},{14,10},{7,3},{... | collective-permute-start | bytes 3145736 | tf_op jit(solution)/shard_map/ppermute | solution.py:267
  47.0 172.9 %copy-start.27 = (f32[1,256]{1,0:T(1,128)S(1)}, f32[1,256]{1,0:T(1,128)}, u32[]{:S(2)}) copy-start(f32[1,256]{1,0:T(1,128)} %get-tuple-element.40) | copy-start | bytes 3076
  52.9 16.9 %collective-permute-start.19 = (bf16[128,2048]{1,0:T(8,128)(2,1)S(1)}, bf16[128,2048]{1,0:T(8,128)(2,1)}, u32[]{:S(2)}, u32[]{:S(2)}) collective-permute-start(bf16[128,2048]{1,0:T(8,128)(2,1)S(1)} %divide_convert_fusion.5), channel_id=1, source_target_pairs={{4,0},{8,4},{12,8},{5,1},{9,5},{13,9},{6,2},{10,6},{14,10},{7,3},{... | collective-permute-start | bytes 1572872 | tf_op jit(solution)/shard_map/ppermute | solution.py:267
  54.2 19.6 %collective-permute-start.21 = (bf16[128,2048]{1,0:T(8,128)(2,1)S(1)}, bf16[128,2048]{1,0:T(8,128)(2,1)}, u32[]{:S(2)}, u32[]{:S(2)}) collective-permute-start(bf16[128,2048]{1,0:T(8,128)(2,1)S(1)} %divide_convert_fusion.5), channel_id=1, source_target_pairs={{0,4},{4,8},{8,12},{1,5},{5,9},{9,13},{2,6},{6,10},{10,14},{3,7},{... | collective-permute-start | bytes 1572872 | tf_op jit(solution)/shard_map/ppermute | solution.py:266
  59.6 87.8 %collective-permute-start.15 = (bf16[384,2048]{1,0:T(8,128)(2,1)S(1)}, bf16[384,2048]{1,0:T(8,128)(2,1)S(1)}, u32[]{:S(2)}, u32[]{:S(2)}) collective-permute-start(bf16[384,2048]{1,0:T(8,128)(2,1)S(1)} %divide_convert_fusion.3), channel_id=1, source_target_pairs={{4,0},{8,4},{12,8},{5,1},{9,5},{13,9},{6,2},{10,6},{14,10},{7,3},{... | collective-permute-start | bytes 4718600 | tf_op jit(solution)/shard_map/ppermute | solution.py:267
  60.9 87.8 %collective-permute-start.17 = (bf16[384,2048]{1,0:T(8,128)(2,1)S(1)}, bf16[384,2048]{1,0:T(8,128)(2,1)S(1)}, u32[]{:S(2)}, u32[]{:S(2)}) collective-permute-start(bf16[384,2048]{1,0:T(8,128)(2,1)S(1)} %divide_convert_fusion.3), channel_id=1, source_target_pairs={{0,4},{4,8},{8,12},{1,5},{5,9},{9,13},{2,6},{6,10},{10,14},{3,7},{... | collective-permute-start | bytes 4718600 | tf_op jit(solution)/shard_map/ppermute | solution.py:266
  69.8 57.5 %collective-permute-start.41 = (bf16[2048,256]{1,0:T(8,128)(2,1)S(1)}, bf16[2048,256]{1,0:T(8,128)(2,1)S(1)}, u32[]{:S(2)}, u32[]{:S(2)}) collective-permute-start(bf16[2048,256]{1,0:T(8,128)(2,1)S(1)} %divide_convert_fusion.4), channel_id=1, source_target_pairs={{0,4},{4,8},{8,12},{1,5},{5,9},{9,13},{2,6},{6,10},{10,14},{3,7},{... | collective-permute-start | bytes 3145736 | tf_op jit(solution)/shard_map/ppermute | solution.py:266
  73.8 54.8 %collective-permute-start.33 = (bf16[2048,256]{1,0:T(8,128)(2,1)S(1)}, bf16[2048,256]{1,0:T(8,128)(2,1)S(1)}, u32[]{:S(2)}, u32[]{:S(2)}) collective-permute-start(bf16[2048,256]{1,0:T(8,128)(2,1)S(1)} %copy-done.12), channel_id=1, source_target_pairs={{4,0},{8,4},{12,8},{5,1},{9,5},{13,9},{6,2},{10,6},{14,10},{7,3},{... | collective-permute-start | bytes 3145736 | tf_op jit(solution)/shard_map/ppermute | solution.py:267
  75.1 71.6 %collective-permute-start.35 = (bf16[2048,256]{1,0:T(8,128)(2,1)S(1)}, bf16[2048,256]{1,0:T(8,128)(2,1)}, u32[]{:S(2)}, u32[]{:S(2)}) collective-permute-start(bf16[2048,256]{1,0:T(8,128)(2,1)S(1)} %copy-done.12), channel_id=1, source_target_pairs={{0,4},{4,8},{8,12},{1,5},{5,9},{9,13},{2,6},{6,10},{10,14},{3,7},{... | collective-permute-start | bytes 3145736 | tf_op jit(solution)/shard_map/ppermute | solution.py:266
  127.3 122.0 %collective-permute-start.3 = (bf16[512,2048]{1,0:T(8,128)(2,1)}, bf16[512,2048]{1,0:T(8,128)(2,1)}, u32[]{:S(2)}, u32[]{:S(2)}) collective-permute-start(bf16[512,2048]{1,0:T(8,128)(2,1)} %divide_convert_fusion.2), channel_id=1, source_target_pairs={{4,0},{8,4},{12,8},{5,1},{9,5},{13,9},{6,2},{10,6},{14,10},{7,3},{... | collective-permute-start | bytes 6291464 | tf_op jit(solution)/shard_map/ppermute | solution.py:267
  128.6 72.2 %collective-permute-start.40 = (bf16[2048,256]{1,0:T(8,128)(2,1)}, bf16[2048,256]{1,0:T(8,128)(2,1)S(1)}, u32[]{:S(2)}, u32[]{:S(2)}) collective-permute-start(bf16[2048,256]{1,0:T(8,128)(2,1)} %collective-permute-done.39), channel_id=1, source_target_pairs={{4,0},{8,4},{5,1},{9,5},{6,2},{10,6},{7,3},{11,7},{20,16},{24,20},... | collective-permute-start | bytes 3145736 | tf_op jit(solution)/shard_map/ppermute | solution.py:267
  146.7 59.5 %collective-permute-start.42 = (bf16[2048,256]{1,0:T(8,128)(2,1)S(1)}, bf16[2048,256]{1,0:T(8,128)(2,1)S(1)}, u32[]{:S(2)}, u32[]{:S(2)}) collective-permute-start(bf16[2048,256]{1,0:T(8,128)(2,1)S(1)} %collective-permute-done.41), channel_id=1, source_target_pairs={{4,8},{8,12},{5,9},{9,13},{6,10},{10,14},{7,11},{11,15},{20,24},{2... | collective-permute-start | bytes 3145736 | tf_op jit(solution)/shard_map/ppermute | solution.py:266
  147.4 70.1 %collective-permute-start.34 = (bf16[2048,256]{1,0:T(8,128)(2,1)S(1)}, bf16[2048,256]{1,0:T(8,128)(2,1)S(1)}, u32[]{:S(2)}, u32[]{:S(2)}) collective-permute-start(bf16[2048,256]{1,0:T(8,128)(2,1)S(1)} %collective-permute-done.33), channel_id=1, source_target_pairs={{4,0},{8,4},{5,1},{9,5},{6,2},{10,6},{7,3},{11,7},{20,16},{24,20},... | collective-permute-start | bytes 3145736 | tf_op jit(solution)/shard_map/ppermute | solution.py:267
  148.7 74.1 %collective-permute-start.36 = (bf16[2048,256]{1,0:T(8,128)(2,1)}, bf16[2048,256]{1,0:T(8,128)(2,1)}, u32[]{:S(2)}, u32[]{:S(2)}) collective-permute-start(bf16[2048,256]{1,0:T(8,128)(2,1)} %collective-permute-done.35), channel_id=1, source_target_pairs={{4,8},{8,12},{5,9},{9,13},{6,10},{10,14},{7,11},{11,15},{20,24},{2... | collective-permute-start | bytes 3145736 | tf_op jit(solution)/shard_map/ppermute | solution.py:266
  200.8 60.6 %collective-permute-start.5 = (bf16[512,2048]{1,0:T(8,128)(2,1)}, bf16[512,2048]{1,0:T(8,128)(2,1)}, u32[]{:S(2)}, u32[]{:S(2)}) collective-permute-start(bf16[512,2048]{1,0:T(8,128)(2,1)} %divide_convert_fusion.2), channel_id=1, source_target_pairs={{0,4},{4,8},{8,12},{1,5},{5,9},{9,13},{2,6},{6,10},{10,14},{3,7},{... | collective-permute-start | bytes 6291464 | tf_op jit(solution)/shard_map/ppermute | solution.py:266
  206.2 89.8 %collective-permute-start.9 = (bf16[512,2048]{1,0:T(8,128)(2,1)}, bf16[512,2048]{1,0:T(8,128)(2,1)}, u32[]{:S(2)}, u32[]{:S(2)}) collective-permute-start(bf16[512,2048]{1,0:T(8,128)(2,1)} %divide_convert_fusion.1), channel_id=1, source_target_pairs={{0,4},{4,8},{8,12},{1,5},{5,9},{9,13},{2,6},{6,10},{10,14},{3,7},{... | collective-permute-start | bytes 6291464 | tf_op jit(solution)/shard_map/ppermute | solution.py:266
  218.5 78.8 %collective-permute-start.7 = (bf16[512,2048]{1,0:T(8,128)(2,1)}, bf16[512,2048]{1,0:T(8,128)(2,1)}, u32[]{:S(2)}, u32[]{:S(2)}) collective-permute-start(bf16[512,2048]{1,0:T(8,128)(2,1)} %divide_convert_fusion.1), channel_id=1, source_target_pairs={{4,0},{8,4},{12,8},{5,1},{9,5},{13,9},{6,2},{10,6},{14,10},{7,3},{... | collective-permute-start | bytes 6291464 | tf_op jit(solution)/shard_map/ppermute | solution.py:267
  222.8 91.3 %collective-permute-start.11 = (bf16[512,2048]{1,0:T(8,128)(2,1)S(1)}, bf16[512,2048]{1,0:T(8,128)(2,1)}, u32[]{:S(2)}, u32[]{:S(2)}) collective-permute-start(bf16[512,2048]{1,0:T(8,128)(2,1)S(1)} %divide_convert_fusion), channel_id=1, source_target_pairs={{4,0},{8,4},{12,8},{5,1},{9,5},{13,9},{6,2},{10,6},{14,10},{7,3},{... | collective-permute-start | bytes 6291464 | tf_op jit(solution)/shard_map/ppermute | solution.py:267
  249.3 76.6 %collective-permute-start.13 = (bf16[512,2048]{1,0:T(8,128)(2,1)S(1)}, bf16[512,2048]{1,0:T(8,128)(2,1)S(1)}, u32[]{:S(2)}, u32[]{:S(2)}) collective-permute-start(bf16[512,2048]{1,0:T(8,128)(2,1)S(1)} %divide_convert_fusion), channel_id=1, source_target_pairs={{0,4},{4,8},{8,12},{1,5},{5,9},{9,13},{2,6},{6,10},{10,14},{3,7},{... | collective-permute-start | bytes 6291464 | tf_op jit(solution)/shard_map/ppermute | solution.py:266
  261.5 65.7 %collective-permute-start.43 = (bf16[2048,256]{1,0:T(8,128)(2,1)S(1)}, bf16[2048,256]{1,0:T(8,128)(2,1)S(1)}, u32[]{:S(2)}, u32[]{:S(2)}) collective-permute-start(bf16[2048,256]{1,0:T(8,128)(2,1)S(1)} %copy-done.23), channel_id=1, source_target_pairs={{8,12},{9,13},{10,14},{11,15},{24,28},{25,29},{26,30},{27,31}} | collective-permute-start | bytes 3145736 | tf_op jit(solution)/shard_map/ppermute | solution.py:266
  296.0 40.5 %collective-permute-start.44 = (bf16[2048,256]{1,0:T(8,128)(2,1)S(1)}, bf16[2048,256]{1,0:T(8,128)(2,1)S(1)}, u32[]{:S(2)}, u32[]{:S(2)}) collective-permute-start(bf16[2048,256]{1,0:T(8,128)(2,1)S(1)} %copy-done.21), channel_id=1, source_target_pairs={{4,0},{5,1},{6,2},{7,3},{20,16},{21,17},{22,18},{23,19}} | collective-permute-start | bytes 3145736 | tf_op jit(solution)/shard_map/ppermute | solution.py:267
  297.3 107.9 %collective-permute-start.4 = (bf16[512,2048]{1,0:T(8,128)(2,1)}, bf16[512,2048]{1,0:T(8,128)(2,1)S(1)}, u32[]{:S(2)}, u32[]{:S(2)}) collective-permute-start(bf16[512,2048]{1,0:T(8,128)(2,1)} %collective-permute-done.3), channel_id=1, source_target_pairs={{4,0},{8,4},{5,1},{9,5},{6,2},{10,6},{7,3},{11,7},{20,16},{24,20},... | collective-permute-start | bytes 6291464 | tf_op jit(solution)/shard_map/ppermute | solution.py:267
  299.0 107.1 %copy-start.15 = (bf16[2048,256]{1,0:T(8,128)(2,1)S(1)}, bf16[2048,256]{1,0:T(8,128)(2,1)}, u32[]{:S(2)}) copy-start(bf16[2048,256]{1,0:T(8,128)(2,1)} %copy-done.14) | copy-start | bytes 3145732
  314.2 24.9 %collective-permute-start.37 = (bf16[2048,256]{1,0:T(8,128)(2,1)}, bf16[2048,256]{1,0:T(8,128)(2,1)S(1)}, u32[]{:S(2)}, u32[]{:S(2)}) collective-permute-start(bf16[2048,256]{1,0:T(8,128)(2,1)} %collective-permute-done.36), channel_id=1, source_target_pairs={{8,12},{9,13},{10,14},{11,15},{24,28},{25,29},{26,30},{27,31}} | collective-permute-start | bytes 3145736 | tf_op jit(solution)/shard_map/ppermute | solution.py:266
  325.9 78.1 %collective-permute-start.38 = (bf16[2048,256]{1,0:T(8,128)(2,1)S(1)}, bf16[2048,256]{1,0:T(8,128)(2,1)S(1)}, u32[]{:S(2)}, u32[]{:S(2)}) collective-permute-start(bf16[2048,256]{1,0:T(8,128)(2,1)S(1)} %copy-done.19), channel_id=1, source_target_pairs={{4,0},{5,1},{6,2},{7,3},{20,16},{21,17},{22,18},{23,19}} | collective-permute-start | bytes 3145736 | tf_op jit(solution)/shard_map/ppermute | solution.py:267
  327.2 80.6 %collective-permute-start.6 = (bf16[512,2048]{1,0:T(8,128)(2,1)}, bf16[512,2048]{1,0:T(8,128)(2,1)S(1)}, u32[]{:S(2)}, u32[]{:S(2)}) collective-permute-start(bf16[512,2048]{1,0:T(8,128)(2,1)} %collective-permute-done.5), channel_id=1, source_target_pairs={{4,8},{8,12},{5,9},{9,13},{6,10},{10,14},{7,11},{11,15},{20,24},{2... | collective-permute-start | bytes 6291464 | tf_op jit(solution)/shard_map/ppermute | solution.py:266
  336.5 72.5 %collective-permute-start.10 = (bf16[512,2048]{1,0:T(8,128)(2,1)}, bf16[512,2048]{1,0:T(8,128)(2,1)S(1)}, u32[]{:S(2)}, u32[]{:S(2)}) collective-permute-start(bf16[512,2048]{1,0:T(8,128)(2,1)} %collective-permute-done.9), channel_id=1, source_target_pairs={{4,8},{8,12},{5,9},{9,13},{6,10},{10,14},{7,11},{11,15},{20,24},{2... | collective-permute-start | bytes 6291464 | tf_op jit(solution)/shard_map/ppermute | solution.py:266
  339.0 109.9 %collective-permute-start.8 = (bf16[512,2048]{1,0:T(8,128)(2,1)}, bf16[512,2048]{1,0:T(8,128)(2,1)S(1)}, u32[]{:S(2)}, u32[]{:S(2)}) collective-permute-start(bf16[512,2048]{1,0:T(8,128)(2,1)} %collective-permute-done.7), channel_id=1, source_target_pairs={{4,0},{8,4},{5,1},{9,5},{6,2},{10,6},{7,3},{11,7},{20,16},{24,20},... | collective-permute-start | bytes 6291464 | tf_op jit(solution)/shard_map/ppermute | solution.py:267
  403.9 89.9 %collective-permute-start.12 = (bf16[512,2048]{1,0:T(8,128)(2,1)}, bf16[512,2048]{1,0:T(8,128)(2,1)S(1)}, u32[]{:S(2)}, u32[]{:S(2)}) collective-permute-start(bf16[512,2048]{1,0:T(8,128)(2,1)} %collective-permute-done.11), channel_id=1, source_target_pairs={{4,0},{8,4},{5,1},{9,5},{6,2},{10,6},{7,3},{11,7},{20,16},{24,20},... | collective-permute-start | bytes 6291464 | tf_op jit(solution)/shard_map/ppermute | solution.py:267
  405.2 89.3 %collective-permute-start.14 = (bf16[512,2048]{1,0:T(8,128)(2,1)S(1)}, bf16[512,2048]{1,0:T(8,128)(2,1)S(1)}, u32[]{:S(2)}, u32[]{:S(2)}) collective-permute-start(bf16[512,2048]{1,0:T(8,128)(2,1)S(1)} %collective-permute-done.13), channel_id=1, source_target_pairs={{4,8},{8,12},{5,9},{9,13},{6,10},{10,14},{7,11},{11,15},{20,24},{2... | collective-permute-start | bytes 6291464 | tf_op jit(solution)/shard_map/ppermute | solution.py:266
  406.3 124.5 %copy-start.5 = (bf16[8192,256]{1,0:T(8,128)(2,1)}, bf16[8192,256]{1,0:T(8,128)(2,1)S(1)}, u32[]{:S(2)}) copy-start(bf16[8192,256]{1,0:T(8,128)(2,1)S(1)} %select_dynamic-update-slice_fusion.12) | copy-start | bytes 12582916
  407.7 119.8 %collective-permute-start.16 = (bf16[384,2048]{1,0:T(8,128)(2,1)S(1)}, bf16[384,2048]{1,0:T(8,128)(2,1)S(1)}, u32[]{:S(2)}, u32[]{:S(2)}) collective-permute-start(bf16[384,2048]{1,0:T(8,128)(2,1)S(1)} %copy-done.11), channel_id=1, source_target_pairs={{4,0},{8,4},{5,1},{9,5},{6,2},{10,6},{7,3},{11,7},{20,16},{24,20},... | collective-permute-start | bytes 4718600 | tf_op jit(solution)/shard_map/ppermute | solution.py:267
  409.1 119.2 %collective-permute-start.18 = (bf16[384,2048]{1,0:T(8,128)(2,1)S(1)}, bf16[384,2048]{1,0:T(8,128)(2,1)S(1)}, u32[]{:S(2)}, u32[]{:S(2)}) collective-permute-start(bf16[384,2048]{1,0:T(8,128)(2,1)S(1)} %copy-done.9), channel_id=1, source_target_pairs={{4,8},{8,12},{5,9},{9,13},{6,10},{10,14},{7,11},{11,15},{20,24},{2... | collective-permute-start | bytes 4718600 | tf_op jit(solution)/shard_map/ppermute | solution.py:266
  448.9 129.4 %collective-permute-start.23 = (bf16[512,2048]{1,0:T(8,128)(2,1)S(1)}, bf16[512,2048]{1,0:T(8,128)(2,1)S(1)}, u32[]{:S(2)}, u32[]{:S(2)}) collective-permute-start(bf16[512,2048]{1,0:T(8,128)(2,1)S(1)} %collective-permute-done.6), channel_id=1, source_target_pairs={{8,12},{9,13},{10,14},{11,15},{24,28},{25,29},{26,30},{27,31}} | collective-permute-start | bytes 6291464 | tf_op jit(solution)/shard_map/ppermute | solution.py:266
  493.8 4.1 collective-permute-start.22
  494.5 88.3 %collective-permute-start.24 = (bf16[512,2048]{1,0:T(8,128)(2,1)S(1)}, bf16[512,2048]{1,0:T(8,128)(2,1)S(1)}, u32[]{:S(2)}, u32[]{:S(2)}) collective-permute-start(bf16[512,2048]{1,0:T(8,128)(2,1)S(1)} %collective-permute-done.4), channel_id=1, source_target_pairs={{4,0},{5,1},{6,2},{7,3},{20,16},{21,17},{22,18},{23,19}} | collective-permute-start | bytes 6291464 | tf_op jit(solution)/shard_map/ppermute | solution.py:267
  497.9 78.1 %collective-permute-start.20 = (bf16[128,2048]{1,0:T(8,128)(2,1)}, bf16[128,2048]{1,0:T(8,128)(2,1)S(1)}, u32[]{:S(2)}, u32[]{:S(2)}) collective-permute-start(bf16[128,2048]{1,0:T(8,128)(2,1)} %collective-permute-done.19), channel_id=1, source_target_pairs={{4,0},{8,4},{5,1},{9,5},{6,2},{10,6},{7,3},{11,7},{20,16},{24,20},... | collective-permute-start | bytes 1572872 | tf_op jit(solution)/shard_map/ppermute | solution.py:267
  527.5 211.2 %collective-permute-start.31 = (bf16[128,2048]{1,0:T(8,128)(2,1)S(1)}, bf16[128,2048]{1,0:T(8,128)(2,1)S(1)}, u32[]{:S(2)}, u32[]{:S(2)}) collective-permute-start(bf16[128,2048]{1,0:T(8,128)(2,1)S(1)} %collective-permute-done.22), channel_id=1, source_target_pairs={{8,12},{9,13},{10,14},{11,15},{24,28},{25,29},{26,30},{27,31}} | collective-permute-start | bytes 1572872 | tf_op jit(solution)/shard_map/ppermute | solution.py:266
  528.2 57.9 %collective-permute-start.25 = (bf16[512,2048]{1,0:T(8,128)(2,1)S(1)}, bf16[512,2048]{1,0:T(8,128)(2,1)S(1)}, u32[]{:S(2)}, u32[]{:S(2)}) collective-permute-start(bf16[512,2048]{1,0:T(8,128)(2,1)S(1)} %collective-permute-done.10), channel_id=1, source_target_pairs={{8,12},{9,13},{10,14},{11,15},{24,28},{25,29},{26,30},{27,31}} | collective-permute-start | bytes 6291464 | tf_op jit(solution)/shard_map/ppermute | solution.py:266
  576.1 85.3 %collective-permute-start.26 = (bf16[512,2048]{1,0:T(8,128)(2,1)S(1)}, bf16[512,2048]{1,0:T(8,128)(2,1)S(1)}, u32[]{:S(2)}, u32[]{:S(2)}) collective-permute-start(bf16[512,2048]{1,0:T(8,128)(2,1)S(1)} %collective-permute-done.8), channel_id=1, source_target_pairs={{4,0},{5,1},{6,2},{7,3},{20,16},{21,17},{22,18},{23,19}} | collective-permute-start | bytes 6291464 | tf_op jit(solution)/shard_map/ppermute | solution.py:267
  578.3 86.0 %collective-permute-start.27 = (bf16[512,2048]{1,0:T(8,128)(2,1)S(1)}, bf16[512,2048]{1,0:T(8,128)(2,1)S(1)}, u32[]{:S(2)}, u32[]{:S(2)}) collective-permute-start(bf16[512,2048]{1,0:T(8,128)(2,1)S(1)} %collective-permute-done.14), channel_id=1, source_target_pairs={{8,12},{9,13},{10,14},{11,15},{24,28},{25,29},{26,30},{27,31}} | collective-permute-start | bytes 6291464 | tf_op jit(solution)/shard_map/ppermute | solution.py:266
  582.8 123.5 %collective-permute-start.28 = (bf16[512,2048]{1,0:T(8,128)(2,1)S(1)}, bf16[512,2048]{1,0:T(8,128)(2,1)S(1)}, u32[]{:S(2)}, u32[]{:S(2)}) collective-permute-start(bf16[512,2048]{1,0:T(8,128)(2,1)S(1)} %collective-permute-done.12), channel_id=1, source_target_pairs={{4,0},{5,1},{6,2},{7,3},{20,16},{21,17},{22,18},{23,19}} | collective-permute-start | bytes 6291464 | tf_op jit(solution)/shard_map/ppermute | solution.py:267
  586.2 154.5 %collective-permute-start.32 = (bf16[128,2048]{1,0:T(8,128)(2,1)S(1)}, bf16[128,2048]{1,0:T(8,128)(2,1)S(1)}, u32[]{:S(2)}, u32[]{:S(2)}) collective-permute-start(bf16[128,2048]{1,0:T(8,128)(2,1)S(1)} %collective-permute-done.20), channel_id=1, source_target_pairs={{4,0},{5,1},{6,2},{7,3},{20,16},{21,17},{22,18},{23,19}} | collective-permute-start | bytes 1572872 | tf_op jit(solution)/shard_map/ppermute | solution.py:267
  661.4 47.1 %collective-permute-start.29 = (bf16[384,2048]{1,0:T(8,128)(2,1)S(1)}, bf16[384,2048]{1,0:T(8,128)(2,1)S(1)}, u32[]{:S(2)}, u32[]{:S(2)}) collective-permute-start(bf16[384,2048]{1,0:T(8,128)(2,1)S(1)} %collective-permute-done.18), channel_id=1, source_target_pairs={{8,12},{9,13},{10,14},{11,15},{24,28},{25,29},{26,30},{27,31}} | collective-permute-start | bytes 4718600 | tf_op jit(solution)/shard_map/ppermute | solution.py:266
  664.2 72.8 %collective-permute-start.30 = (bf16[384,2048]{1,0:T(8,128)(2,1)S(1)}, bf16[384,2048]{1,0:T(8,128)(2,1)S(1)}, u32[]{:S(2)}, u32[]{:S(2)}) collective-permute-start(bf16[384,2048]{1,0:T(8,128)(2,1)S(1)} %collective-permute-done.16), channel_id=1, source_target_pairs={{4,0},{5,1},{6,2},{7,3},{20,16},{21,17},{22,18},{23,19}} | collective-permute-start | bytes 4718600 | tf_op jit(solution)/shard_map/ppermute | solution.py:267
  (25 other events, 805.9 us)
where the time goes:
time: 743 us; the launch traced here: 742 us
  waiting for transfers between devices  543 us (73%)
  starting transfers between devices  76.1 us (10%)
  other arithmetic  71.9 us (10%)
  local copies, waits for them, and re-layouts  30.4 us (4%)
  Pallas kernels  18.3 us (2%)
    ppermute x21, waiting for transfers between devices, send(): below = lax.ppermute(block[1], 'zero', down[hop])  436 us
    ppermute x21, waiting for transfers between devices, send(): above = lax.ppermute(block[0], 'zero', up[hop])  107 us
    ppermute x21, starting transfers between devices, send(): above = lax.ppermute(block[0], 'zero', up[hop])  44.7 us
    dynamic_update_slice x21, other arithmetic, place(): lax.dynamic_update_slice(serve[which], block, (owner * rows + low, jnp.ze...  38.8 us
    ppermute x21, starting transfers between devices, send(): below = lax.ppermute(block[1], 'zero', down[hop])  27.5 us
    convert_element_type x6, other arithmetic, narrow(): block = (fresh_of(which, low, high) / scale).astype(jnp.bfloat16)  21.4 us
  transfers between devices with their start and end apart: 45, of which 19 were waited for; matrix products, arithmetic and copies ran while one was open for 11% of the time, Pallas kernels for 1%

commit v1 on v0

--- a/solution.py
+++ b/solution.py
@@ -246,8 +246,6 @@
 ):
     rows = mix_share.shape[0]
     z = lax.axis_index("zero")
-    up = [[(k, k + 1) for k in range(hop, n_zero - 1)] for hop in range(n_zero - 1)]
-    down = [[(k, k - 1) for k in range(1, n_zero - hop)] for hop in range(n_zero - 1)]
     ring = [[(k, (k + shift) % n_zero) for k in range(n_zero)] for shift in range(n_zero)]
 
     key_block, key_total, value_total, gain = lead(
@@ -262,12 +260,10 @@
     )
     factors = [None, jnp.sqrt(key_total[0]), jnp.sqrt(value_total[0])]
 
-    def send(block, hop):
-        above = lax.ppermute(block[0], "zero", up[hop])
-        below = lax.ppermute(block[1], "zero", down[hop])
-        return above, below
-
-    key_moved = send((key_block, key_block), 0)
+    def send(block):
+        return lax.ppermute(block, "zero", ring[1])
+
+    key_moved = send(key_block)
     first_query, second_query, first_value, second_value, share, _ = lax.optimization_barrier(
         (first_query, second_query, first_value, second_value, mix_share, key_block)
     )
@@ -310,23 +306,16 @@
     widths = [first_query.shape[1], first_key.shape[1], first_value.shape[1]]
     serve = [jnp.zeros((n_zero * rows, width), jnp.bfloat16) for width in widths]
 
-    def place(piece, block, owner):
-        which, low, _ = piece
-        serve[which] = lax.dynamic_update_slice(serve[which], block, (owner * rows + low, jnp.zeros_like(owner)))
-
-    for piece, block in zip(pieces, blocks):
-        place(piece, block, z)
-    above, below = {}, {}
-    flying = [(block, block) for block in blocks]
-    for hop in range(n_zero - 1):
-        for k, piece in enumerate(pieces):
-            flying[k] = key_moved if (hop, k) == (0, 0) else send(flying[k], hop)
-            above[hop + 1, k], below[hop + 1, k] = flying[k]
-        for k, piece in enumerate(pieces):
-            for away in range(1, n_zero):
-                if max(away, n_zero - away) == hop + 1:
-                    block = jnp.where(z + away < n_zero, below[away, k], above[n_zero - away, k])
-                    place(piece, block, lax.rem(z + away, n_zero))
+    for hop in range(n_zero):
+        owner = lax.rem(z + n_zero - hop, n_zero)
+        moved = []
+        for k, ((which, low, _), block) in enumerate(zip(pieces, blocks)):
+            if hop < n_zero - 1:
+                moved.append(key_moved if (hop, k) == (0, 0) else send(block))
+            serve[which] = lax.dynamic_update_slice(
+                serve[which], block, (owner * rows + low, jnp.zeros_like(owner))
+            )
+        blocks = moved
     gain = gain.reshape(n_model, n_zero, -1).transpose(1, 0, 2)
     return (*serve, *factors, gain.reshape(-1))
 

time: 743 us -> 713 us (0.960)
  starting transfers between devices: 76.1 us -> 13.8 us
  local copies, waits for them, and re-layouts: 30.4 us -> 71.5 us
  other arithmetic: 71.9 us -> 33.8 us
  waiting for transfers between devices: 543 us -> 574 us
    ppermute x42 -> x21, starting transfers between devices: 72.2 us -> 9.9 us  [send(): return lax.ppermute(block, 'zero', ring[1])]
    dynamic_update_slice x7 -> x28, local copies, waits for them, and re-layouts: 11 us -> 52.2 us  [merge(): lax.dynamic_update_slice(serve[which], block, (owner * rows + low, jnp.ze...]
    dynamic_update_slice x21 -> x0, other arithmetic: 38.8 us -> none  [place(): lax.dynamic_update_slice(serve[which], block, (owner * rows + low, jnp.ze...]
    ppermute x42 -> x21, waiting for transfers between devices: 543 us -> 574 us  [send(): return lax.ppermute(block, 'zero', ring[1])]
  transfers between devices with their start and end apart: 45 -> 24, of which waited for: 19 -> 11; matrix products, arithmetic and copies ran while one was open for 11% -> 13% of each run, Pallas kernels for 1% -> 1%
where the time goes in v1:
time: 713 us; the launch traced here: 712 us
  waiting for transfers between devices  574 us (81%)
  local copies, waits for them, and re-layouts  71.5 us (10%)
  other arithmetic  33.8 us (5%)
  Pallas kernels  18.3 us (3%)
  starting transfers between devices  13.8 us (2%)
    ppermute x21, waiting for transfers between devices, send(): return lax.ppermute(block, 'zero', ring[1])  574 us
    dynamic_update_slice x28, local copies, waits for them, and re-layouts, merge(): lax.dynamic_update_slice(serve[which], block, (owner * rows + low, jnp.ze...  52.2 us
    convert_element_type x6, other arithmetic, narrow(): block = (fresh_of(which, low, high) / scale).astype(jnp.bfloat16)  22 us
  transfers between devices with their start and end apart: 24, of which 11 were waited for; matrix products, arithmetic and copies ran while one was open for 13% of the time, Pallas kernels for 1%

profile of v1, /device:TPU:0, one launch (start us, length us, event | category | flops | bytes accessed | tf_op | source)
XLA Modules:
  0.0 712.5 jit_solution(10945765805074241517)
XLA Ops:
  0.7 12.2 %lead.1 = (bf16[2048,256]{1,0:T(8,128)(2,1)}, f32[1,256]{1,0:T(1,128)}, f32[1,256]{1,0:T(1,128)}, bf16[4,1,512]{2,1,0:T(2,128)(2,1)}) custom-call(f32[2048,256]{1,0:T(8,128)} %first_key.1, f32[2048,256]{1,0:T(8,128)} %second_key.1, f32[2048,256]{1,0:T(8,128)} %first_value.1, f32[2048,256]{1,0:T(8,128)} %second_value.1, f32[16,128]{1,0:T(8,128)} %bitcast.24, ...), custom_call_target="tpu_custom_call" | custom-call | tf_op jit(solution)/shard_map/lead/pallas_call | solution.py:151
  13.6 1.9 divide_convert_fusion.4
  15.5 11.6 %multiply_reduce_fusion = f32[2048]{0:T(1024)S(1)} fusion(f32[2048,2048]{1,0:T(8,128)} %param.10, f32[2048,2048]{1,0:T(8,128)} %param.9, f32[2048]{0:T(1024)S(1)} %broadcast_subtract_fusion, f32[2048]{0:T(1024)S(1)} %copy-done.9), kind=kLoop, calls=%fused_computation | loop fusion | flops 20969472 | bytes 33579008 | tf_op jit(solution)/shard_map/reduce_sum | solution.py:286
  27.8 1.2 collective-permute-start.1
  29.0 2.0 collective-permute-start.2
  31.6 2.0 collective-permute-start.21
  33.9 4.9 divide_convert_fusion.2
  38.8 2.3 collective-permute-start.3
  41.1 5.0 divide_convert_fusion.1
  46.1 3.9 divide_convert_fusion
  50.0 4.5 divide_convert_fusion.3
  54.5 1.8 divide_convert_fusion.5
  56.4 1.6 collective-permute-start.4
  58.0 79.8 %collective-permute-done.7 = bf16[128,2048]{1,0:T(8,128)(2,1)S(1)} collective-permute-done((bf16[128,2048]{1,0:T(8,128)(2,1)S(1)}, bf16[128,2048]{1,0:T(8,128)(2,1)S(1)}, u32[]{:S(2)}, u32[]{:S(2)}) %collective-permute-start.7) | collective-permute-done | bytes 524320 | tf_op jit(solution)/shard_map/ppermute | solution.py:264
  139.9 2.3 broadcast.38.clone.1
  143.3 2.3 broadcast.38.clone
  145.6 2.3 constant_dynamic-update-slice_fusion.4
  147.9 11.2 %broadcast_in_dim.6 = bf16[8192,2048]{1,0:T(8,128)(2,1)} broadcast(bf16[]{:T(256)} %constant.61.clone.1), dimensions={} | broadcast | bytes 33554432 | tf_op jit(solution)/shard_map/broadcast_in_dim | solution.py:307
  159.0 3.2 constant_dynamic-update-slice_fusion.24
  162.2 96.7 %collective-permute-done.12 = bf16[128,2048]{1,0:T(8,128)(2,1)S(1)} collective-permute-done((bf16[128,2048]{1,0:T(8,128)(2,1)S(1)}, bf16[128,2048]{1,0:T(8,128)(2,1)S(1)}, u32[]{:S(2)}, u32[]{:S(2)}) %collective-permute-start.12) | collective-permute-done | bytes 524320 | tf_op jit(solution)/shard_map/ppermute | solution.py:264
  258.9 3.2 constant_dynamic-update-slice_fusion.23
  262.7 1.5 constant_dynamic-update-slice_fusion.22
  264.5 2.7 constant_dynamic-update-slice_fusion.21
  267.2 6.1 spread.1
  275.7 11.3 %collective-permute-done.19 = bf16[2048,256]{1,0:T(8,128)(2,1)} collective-permute-done((bf16[2048,256]{1,0:T(8,128)(2,1)}, bf16[2048,256]{1,0:T(8,128)(2,1)}, u32[]{:S(2)}, u32[]{:S(2)}) %collective-permute-start.19) | collective-permute-done | bytes 1048608 | tf_op jit(solution)/shard_map/ppermute | solution.py:264
  287.0 2.3 constant_dynamic-update-slice_fusion.27
  290.0 2.3 constant_dynamic-update-slice_fusion.3
  293.3 2.3 constant_dynamic-update-slice_fusion.2
  295.5 25.2 %collective-permute-done.6 = bf16[384,2048]{1,0:T(8,128)(2,1)} collective-permute-done((bf16[384,2048]{1,0:T(8,128)(2,1)}, bf16[384,2048]{1,0:T(8,128)(2,1)}, u32[]{:S(2)}, u32[]{:S(2)}) %collective-permute-start.6) | collective-permute-done | bytes 1572896 | tf_op jit(solution)/shard_map/ppermute | solution.py:264
  320.7 3.2 constant_dynamic-update-slice_fusion.19
  323.9 64.1 %collective-permute-done.23 = bf16[2048,256]{1,0:T(8,128)(2,1)S(1)} collective-permute-done((bf16[2048,256]{1,0:T(8,128)(2,1)}, bf16[2048,256]{1,0:T(8,128)(2,1)S(1)}, u32[]{:S(2)}, u32[]{:S(2)}) %collective-permute-start.23) | collective-permute-done | bytes 1048608 | tf_op jit(solution)/shard_map/ppermute | solution.py:264
  388.0 3.2 constant_dynamic-update-slice_fusion.18
  391.2 3.2 constant_dynamic-update-slice_fusion.17
  394.4 2.7 constant_dynamic-update-slice_fusion.16
  398.0 35.0 %collective-permute-done.9 = bf16[512,2048]{1,0:T(8,128)(2,1)S(1)} collective-permute-done((bf16[512,2048]{1,0:T(8,128)(2,1)}, bf16[512,2048]{1,0:T(8,128)(2,1)S(1)}, u32[]{:S(2)}, u32[]{:S(2)}) %collective-permute-start.9) | collective-permute-done | bytes 2097184 | tf_op jit(solution)/shard_map/ppermute | solution.py:264
  434.0 100.1 %collective-permute-done.20 = bf16[2048,256]{1,0:T(8,128)(2,1)S(1)} collective-permute-done((bf16[2048,256]{1,0:T(8,128)(2,1)}, bf16[2048,256]{1,0:T(8,128)(2,1)S(1)}, u32[]{:S(2)}, u32[]{:S(2)}) %collective-permute-start.20) | collective-permute-done | bytes 1048608 | tf_op jit(solution)/shard_map/ppermute | solution.py:264
  535.9 3.2 constant_dynamic-update-slice_fusion.14
  539.1 1.5 constant_dynamic-update-slice_fusion.13
  540.5 1.5 constant_dynamic-update-slice_fusion.12
  542.0 1.2 constant_dynamic-update-slice_fusion.11
  544.1 35.0 %collective-permute-done.13 = bf16[512,2048]{1,0:T(8,128)(2,1)S(1)} collective-permute-done((bf16[512,2048]{1,0:T(8,128)(2,1)}, bf16[512,2048]{1,0:T(8,128)(2,1)S(1)}, u32[]{:S(2)}, u32[]{:S(2)}) %collective-permute-start.13) | collective-permute-done | bytes 2097184 | tf_op jit(solution)/shard_map/ppermute | solution.py:264
  579.0 1.5 constant_dynamic-update-slice_fusion.9
  580.5 43.5 %collective-permute-done.14 = bf16[512,2048]{1,0:T(8,128)(2,1)S(1)} collective-permute-done((bf16[512,2048]{1,0:T(8,128)(2,1)S(1)}, bf16[512,2048]{1,0:T(8,128)(2,1)S(1)}, u32[]{:S(2)}, u32[]{:S(2)}) %collective-permute-start.14) | collective-permute-done | bytes 2097184 | tf_op jit(solution)/shard_map/ppermute | solution.py:264
  624.0 1.5 constant_dynamic-update-slice_fusion.8
  625.4 54.7 %collective-permute-done.15 = bf16[512,2048]{1,0:T(8,128)(2,1)S(1)} collective-permute-done((bf16[512,2048]{1,0:T(8,128)(2,1)S(1)}, bf16[512,2048]{1,0:T(8,128)(2,1)S(1)}, u32[]{:S(2)}, u32[]{:S(2)}) %collective-permute-start.15) | collective-permute-done | bytes 2097184 | tf_op jit(solution)/shard_map/ppermute | solution.py:264
  680.1 1.5 constant_dynamic-update-slice_fusion.7
  681.6 28.8 %collective-permute-done.16 = bf16[384,2048]{1,0:T(8,128)(2,1)S(1)} collective-permute-done((bf16[384,2048]{1,0:T(8,128)(2,1)S(1)}, bf16[384,2048]{1,0:T(8,128)(2,1)S(1)}, u32[]{:S(2)}, u32[]{:S(2)}) %collective-permute-start.16) | collective-permute-done | bytes 1572896 | tf_op jit(solution)/shard_map/ppermute | solution.py:264
  710.4 1.2 constant_dynamic-update-slice_fusion.6
  (74 shorter events, 15.7 us)
Async XLA Ops:
  0.6 12.2 %copy-start.9 = (f32[2048]{0:T(1024)S(1)}, f32[2048]{0:T(1024)}, u32[]{:S(2)}) copy-start(f32[2048]{0:T(1024)} %param.15) | copy-start | bytes 24580
  0.6 12.9 %copy-start = (f32[2048,256]{1,0:T(8,128)S(1)}, f32[2048,256]{1,0:T(8,128)}, u32[]{:S(2)}) copy-start(f32[2048,256]{1,0:T(8,128)} %first_value.1) | copy-start | bytes 6291460
  13.6 13.6 %copy-start.10 = (f32[1,256]{1,0:T(1,128)}, f32[1,256]{1,0:T(1,128)S(1)}, u32[]{:S(2)}) copy-start(f32[1,256]{1,0:T(1,128)S(1)} %sqrt.17) | copy-start | bytes 3076
  27.2 6.5 collective-permute-start
  27.8 5.9 collective-permute-start.1
  29.0 4.7 collective-permute-start.2
  31.1 112.2 %collective-permute-start.18 = (bf16[2048,256]{1,0:T(8,128)(2,1)}, bf16[2048,256]{1,0:T(8,128)(2,1)}, u32[]{:S(2)}, u32[]{:S(2)}) collective-permute-start(bf16[2048,256]{1,0:T(8,128)(2,1)} %get-tuple-element.25), channel_id=1, source_target_pairs={{0,4},{4,8},{8,12},{12,0},{1,5},{5,9},{9,13},{13,1},{2,6},{6,10},{... | collective-permute-start | bytes 3145736 | tf_op jit(solution)/shard_map/ppermute | solution.py:264
  31.6 107.5 %collective-permute-start.21 = (bf16[2048,256]{1,0:T(8,128)(2,1)S(1)}, bf16[2048,256]{1,0:T(8,128)(2,1)}, u32[]{:S(2)}, u32[]{:S(2)}) collective-permute-start(bf16[2048,256]{1,0:T(8,128)(2,1)S(1)} %divide_convert_fusion.4), channel_id=1, source_target_pairs={{0,4},{4,8},{8,12},{12,0},{1,5},{5,9},{9,13},{13,1},{2,6},{6,10},{... | collective-permute-start | bytes 3145736 | tf_op jit(solution)/shard_map/ppermute | solution.py:264
  33.8 20.7 %copy-start.8 = (f32[1,2048]{1,0:T(1,128)}, f32[1,2048]{1,0:T(1,128)S(1)}, u32[]{:S(2)}) copy-start(f32[1,2048]{1,0:T(1,128)S(1)} %add_sqrt_fusion) | copy-start | bytes 24580
  38.8 225.4 %collective-permute-start.3 = (bf16[512,2048]{1,0:T(8,128)(2,1)}, bf16[512,2048]{1,0:T(8,128)(2,1)}, u32[]{:S(2)}, u32[]{:S(2)}) collective-permute-start(bf16[512,2048]{1,0:T(8,128)(2,1)} %divide_convert_fusion.2), channel_id=1, source_target_pairs={{0,4},{4,8},{8,12},{12,0},{1,5},{5,9},{9,13},{13,1},{2,6},{6,10},{... | collective-permute-start | bytes 6291464 | tf_op jit(solution)/shard_map/ppermute | solution.py:264
  50.0 88.7 %copy-start.11 = (f32[1,256]{1,0:T(1,128)S(1)}, f32[1,256]{1,0:T(1,128)}, u32[]{:S(2)}) copy-start(f32[1,256]{1,0:T(1,128)} %get-tuple-element.40) | copy-start | bytes 3076
  56.3 1.7 copy-start.1
  56.3 81.5 %collective-permute-start.7 = (bf16[128,2048]{1,0:T(8,128)(2,1)S(1)}, bf16[128,2048]{1,0:T(8,128)(2,1)S(1)}, u32[]{:S(2)}, u32[]{:S(2)}) collective-permute-start(bf16[128,2048]{1,0:T(8,128)(2,1)S(1)} %divide_convert_fusion.5), channel_id=1, source_target_pairs={{0,4},{4,8},{8,12},{12,0},{1,5},{5,9},{9,13},{13,1},{2,6},{6,10},{... | collective-permute-start | bytes 1572872 | tf_op jit(solution)/shard_map/ppermute | solution.py:264
  56.4 230.6 %collective-permute-start.4 = (bf16[512,2048]{1,0:T(8,128)(2,1)}, bf16[512,2048]{1,0:T(8,128)(2,1)}, u32[]{:S(2)}, u32[]{:S(2)}) collective-permute-start(bf16[512,2048]{1,0:T(8,128)(2,1)} %divide_convert_fusion.1), channel_id=1, source_target_pairs={{0,4},{4,8},{8,12},{12,0},{1,5},{5,9},{9,13},{13,1},{2,6},{6,10},{... | collective-permute-start | bytes 6291464 | tf_op jit(solution)/shard_map/ppermute | solution.py:264
  137.8 0.8 copy-start.5
  138.6 150.7 %collective-permute-start.5 = (bf16[512,2048]{1,0:T(8,128)(2,1)S(1)}, bf16[512,2048]{1,0:T(8,128)(2,1)}, u32[]{:S(2)}, u32[]{:S(2)}) collective-permute-start(bf16[512,2048]{1,0:T(8,128)(2,1)S(1)} %divide_convert_fusion), channel_id=1, source_target_pairs={{0,4},{4,8},{8,12},{12,0},{1,5},{5,9},{9,13},{13,1},{2,6},{6,10},{... | collective-permute-start | bytes 6291464 | tf_op jit(solution)/shard_map/ppermute | solution.py:264
  139.2 4.1 copy-start.6
  139.2 122.9 %collective-permute-start.22 = (bf16[2048,256]{1,0:T(8,128)(2,1)}, bf16[2048,256]{1,0:T(8,128)(2,1)S(1)}, u32[]{:S(2)}, u32[]{:S(2)}) collective-permute-start(bf16[2048,256]{1,0:T(8,128)(2,1)} %collective-permute-done.21), channel_id=1, source_target_pairs={{0,4},{4,8},{8,12},{12,0},{1,5},{5,9},{9,13},{13,1},{2,6},{6,10},{... | collective-permute-start | bytes 3145736 | tf_op jit(solution)/shard_map/ppermute | solution.py:264
  143.2 115.6 %collective-permute-start.12 = (bf16[128,2048]{1,0:T(8,128)(2,1)S(1)}, bf16[128,2048]{1,0:T(8,128)(2,1)S(1)}, u32[]{:S(2)}, u32[]{:S(2)}) collective-permute-start(bf16[128,2048]{1,0:T(8,128)(2,1)S(1)} %copy-done.6), channel_id=1, source_target_pairs={{0,4},{4,8},{8,12},{12,0},{1,5},{5,9},{9,13},{13,1},{2,6},{6,10},{... | collective-permute-start | bytes 1572872 | tf_op jit(solution)/shard_map/ppermute | solution.py:264
  258.9 28.1 %collective-permute-start.19 = (bf16[2048,256]{1,0:T(8,128)(2,1)}, bf16[2048,256]{1,0:T(8,128)(2,1)}, u32[]{:S(2)}, u32[]{:S(2)}) collective-permute-start(bf16[2048,256]{1,0:T(8,128)(2,1)} %collective-permute-done.18), channel_id=1, source_target_pairs={{0,4},{4,8},{8,12},{12,0},{1,5},{5,9},{9,13},{13,1},{2,6},{6,10},{... | collective-permute-start | bytes 3145736 | tf_op jit(solution)/shard_map/ppermute | solution.py:264
  262.0 12.8 %copy-start.2 = (bf16[128,2048]{1,0:T(8,128)(2,1)S(1)}, bf16[128,2048]{1,0:T(8,128)(2,1)}, u32[]{:S(2)}) copy-start(bf16[128,2048]{1,0:T(8,128)(2,1)} %copy-done.1) | copy-start | bytes 1572868
  262.0 2.1 copy-start.3
  262.0 58.7 %collective-permute-start.6 = (bf16[384,2048]{1,0:T(8,128)(2,1)}, bf16[384,2048]{1,0:T(8,128)(2,1)}, u32[]{:S(2)}, u32[]{:S(2)}) collective-permute-start(bf16[384,2048]{1,0:T(8,128)(2,1)} %divide_convert_fusion.3), channel_id=1, source_target_pairs={{0,4},{4,8},{8,12},{12,0},{1,5},{5,9},{9,13},{13,1},{2,6},{6,10},{... | collective-permute-start | bytes 4718600 | tf_op jit(solution)/shard_map/ppermute | solution.py:264
  264.1 130.3 %collective-permute-start.8 = (bf16[512,2048]{1,0:T(8,128)(2,1)}, bf16[512,2048]{1,0:T(8,128)(2,1)}, u32[]{:S(2)}, u32[]{:S(2)}) collective-permute-start(bf16[512,2048]{1,0:T(8,128)(2,1)} %collective-permute-done.3), channel_id=1, source_target_pairs={{0,4},{4,8},{8,12},{12,0},{1,5},{5,9},{9,13},{13,1},{2,6},{6,10},{... | collective-permute-start | bytes 6291464 | tf_op jit(solution)/shard_map/ppermute | solution.py:264
  273.4 18.9 %copy-start.4 = (bf16[2048,256]{1,0:T(8,128)(2,1)S(1)}, bf16[2048,256]{1,0:T(8,128)(2,1)}, u32[]{:S(2)}) copy-start(bf16[2048,256]{1,0:T(8,128)(2,1)} %copy-done.3) | copy-start | bytes 3145732
  287.0 101.0 %collective-permute-start.23 = (bf16[2048,256]{1,0:T(8,128)(2,1)}, bf16[2048,256]{1,0:T(8,128)(2,1)S(1)}, u32[]{:S(2)}, u32[]{:S(2)}) collective-permute-start(bf16[2048,256]{1,0:T(8,128)(2,1)} %copy-done.3), channel_id=1, source_target_pairs={{0,4},{4,8},{8,12},{12,0},{1,5},{5,9},{9,13},{13,1},{2,6},{6,10},{... | collective-permute-start | bytes 3145736 | tf_op jit(solution)/shard_map/ppermute | solution.py:264
  287.0 145.9 %collective-permute-start.9 = (bf16[512,2048]{1,0:T(8,128)(2,1)}, bf16[512,2048]{1,0:T(8,128)(2,1)S(1)}, u32[]{:S(2)}, u32[]{:S(2)}) collective-permute-start(bf16[512,2048]{1,0:T(8,128)(2,1)} %collective-permute-done.4), channel_id=1, source_target_pairs={{0,4},{4,8},{8,12},{12,0},{1,5},{5,9},{9,13},{13,1},{2,6},{6,10},{... | collective-permute-start | bytes 6291464 | tf_op jit(solution)/shard_map/ppermute | solution.py:264
  289.3 244.8 %collective-permute-start.10 = (bf16[512,2048]{1,0:T(8,128)(2,1)}, bf16[512,2048]{1,0:T(8,128)(2,1)S(1)}, u32[]{:S(2)}, u32[]{:S(2)}) collective-permute-start(bf16[512,2048]{1,0:T(8,128)(2,1)} %collective-permute-done.5), channel_id=1, source_target_pairs={{0,4},{4,8},{8,12},{12,0},{1,5},{5,9},{9,13},{13,1},{2,6},{6,10},{... | collective-permute-start | bytes 6291464 | tf_op jit(solution)/shard_map/ppermute | solution.py:264
  320.7 214.4 %collective-permute-start.11 = (bf16[384,2048]{1,0:T(8,128)(2,1)}, bf16[384,2048]{1,0:T(8,128)(2,1)S(1)}, u32[]{:S(2)}, u32[]{:S(2)}) collective-permute-start(bf16[384,2048]{1,0:T(8,128)(2,1)} %collective-permute-done.6), channel_id=1, source_target_pairs={{0,4},{4,8},{8,12},{12,0},{1,5},{5,9},{9,13},{13,1},{2,6},{6,10},{... | collective-permute-start | bytes 4718600 | tf_op jit(solution)/shard_map/ppermute | solution.py:264
  388.0 146.1 %collective-permute-start.20 = (bf16[2048,256]{1,0:T(8,128)(2,1)}, bf16[2048,256]{1,0:T(8,128)(2,1)S(1)}, u32[]{:S(2)}, u32[]{:S(2)}) collective-permute-start(bf16[2048,256]{1,0:T(8,128)(2,1)} %collective-permute-done.19), channel_id=1, source_target_pairs={{0,4},{4,8},{8,12},{12,0},{1,5},{5,9},{9,13},{13,1},{2,6},{6,10},{... | collective-permute-start | bytes 3145736 | tf_op jit(solution)/shard_map/ppermute | solution.py:264
  391.2 6.0 copy-start.7
  394.4 184.6 %collective-permute-start.13 = (bf16[512,2048]{1,0:T(8,128)(2,1)}, bf16[512,2048]{1,0:T(8,128)(2,1)S(1)}, u32[]{:S(2)}, u32[]{:S(2)}) collective-permute-start(bf16[512,2048]{1,0:T(8,128)(2,1)} %collective-permute-done.8), channel_id=1, source_target_pairs={{0,4},{4,8},{8,12},{12,0},{1,5},{5,9},{9,13},{13,1},{2,6},{6,10},{... | collective-permute-start | bytes 6291464 | tf_op jit(solution)/shard_map/ppermute | solution.py:264
  433.0 191.0 %collective-permute-start.14 = (bf16[512,2048]{1,0:T(8,128)(2,1)S(1)}, bf16[512,2048]{1,0:T(8,128)(2,1)S(1)}, u32[]{:S(2)}, u32[]{:S(2)}) collective-permute-start(bf16[512,2048]{1,0:T(8,128)(2,1)S(1)} %collective-permute-done.9), channel_id=1, source_target_pairs={{0,4},{4,8},{8,12},{12,0},{1,5},{5,9},{9,13},{13,1},{2,6},{6,10},{... | collective-permute-start | bytes 6291464 | tf_op jit(solution)/shard_map/ppermute | solution.py:264
  534.1 177.6 %collective-permute-start.17 = (bf16[128,2048]{1,0:T(8,128)(2,1)S(1)}, bf16[128,2048]{1,0:T(8,128)(2,1)S(1)}, u32[]{:S(2)}, u32[]{:S(2)}) collective-permute-start(bf16[128,2048]{1,0:T(8,128)(2,1)S(1)} %collective-permute-done.12), channel_id=1, source_target_pairs={{0,4},{4,8},{8,12},{12,0},{1,5},{5,9},{9,13},{13,1},{2,6},{6,10},{... | collective-permute-start | bytes 1572872 | tf_op jit(solution)/shard_map/ppermute | solution.py:264
  534.1 146.1 %collective-permute-start.15 = (bf16[512,2048]{1,0:T(8,128)(2,1)S(1)}, bf16[512,2048]{1,0:T(8,128)(2,1)S(1)}, u32[]{:S(2)}, u32[]{:S(2)}) collective-permute-start(bf16[512,2048]{1,0:T(8,128)(2,1)S(1)} %collective-permute-done.10), channel_id=1, source_target_pairs={{0,4},{4,8},{8,12},{12,0},{1,5},{5,9},{9,13},{13,1},{2,6},{6,10},{... | collective-permute-start | bytes 6291464 | tf_op jit(solution)/shard_map/ppermute | solution.py:264
  535.2 175.3 %collective-permute-start.16 = (bf16[384,2048]{1,0:T(8,128)(2,1)S(1)}, bf16[384,2048]{1,0:T(8,128)(2,1)S(1)}, u32[]{:S(2)}, u32[]{:S(2)}) collective-permute-start(bf16[384,2048]{1,0:T(8,128)(2,1)S(1)} %collective-permute-done.11), channel_id=1, source_target_pairs={{0,4},{4,8},{8,12},{12,0},{1,5},{5,9},{9,13},{13,1},{2,6},{6,10},{... | collective-permute-start | bytes 4718600 | tf_op jit(solution)/shard_map/ppermute | solution.py:264
